TPU v7x, 32 devices: a whole 2x2x4 slice. The times are simulated.
32 devices in a mesh: tm: 16 (over z, y, x), rows: 2 (over core).
Axes of the slice: x: 2, y: 2, z: 4, core: 2. Of those that a mesh axis runs over, the one named last changes fastest.
Arguments:
- resid: float32 [2, 16, 16, 512], P(None, 'tm', 'rows'), may hold values from -3 to 3
- basis: float32 [4, 2, 16, 16, 512], P(None, None, 'tm', 'rows'), may hold values from -0.01171875 to 0.01171875
Outputs:
- precond: float32 [2, 16, 16, 512], P(None, 'tm', 'rows')
- image: float32 [2, 16, 16, 512], P(None, 'tm', 'rows')
- gram: float32 [5], replicated
All inputs are finite; a program needn't handle non-finite values.
Results may differ from a plain program's by a relative error of at most 0.0005.
Values sent between devices are 32-bit elements; how exact they have to be, the bound alone decides.
A program may use at most 64 MiB of HBM per device.

v0:
```python
import math
import jax
import jax.numpy as jnp
from jax import lax
from jax.sharding import PartitionSpec as P

SWEEPS = 4
ALPHA = 0.01


def padded_2(shard, sides, width):
    for axis, dim in sides:
        count, length = (lax.axis_size(axis), shard.shape[dim])
        up = [(i, (i + 1) % count) for i in range(count - 1)]
        down = [(j, i) for i, j in up]
        last = lax.slice_in_dim(shard, length - width, length, axis=dim)
        first = lax.slice_in_dim(shard, 0, width, axis=dim)
        before = lax.ppermute(last, axis, up)
        after = lax.ppermute(first, axis, down)
        shard = jnp.concatenate([before, shard, after], axis=dim)
    return shard


def shifted(value, axis, steps):
    count = lax.axis_size(axis)
    first, last = (max(0, -steps), min(count, count - steps))
    return lax.ppermute(value, axis, [(source, source + steps) for source in range(first, last)])


def neighbours(padded):
    middle = padded[:, 1:-1]
    sides = jnp.pad(middle, ((0, 0), (0, 0), (1, 1)))
    return padded[:, 2:] + padded[:, :-2] + sides[:, :, 2:] + sides[:, :, :-2]


def cmul(left, right_re, right_im):
    return jnp.stack(
        [left[0] * right_re - left[1] * right_im, left[0] * right_im + left[1] * right_re]
    )


def phases(first, second, steps):
    turns = first * second % steps
    angle = turns.astype(jnp.float32) * (2.0 * math.pi / steps)
    return (jnp.cos(angle), jnp.sin(angle))


def on_device(resid, basis):
    steps = lax.axis_size("tm")
    coupling = 16.0 / (steps * steps)
    me = lax.axis_index("tm")
    rows_dev = resid.shape[2]
    cols = resid.shape[3]
    cells = rows_dev * cols
    piece = cells // steps
    mine = me.astype(jnp.float32)
    gamma = jnp.power(jnp.float32(ALPHA), mine / steps)
    scaled = resid[:, 0] * gamma
    ordinal = jnp.arange(steps, dtype=jnp.int32)
    cos_table, sin_table = phases(ordinal[:, None], ordinal[None, :], steps)
    blocks = lax.all_to_all(
        scaled.reshape(1, 2, cells), "tm", split_axis=2, concat_axis=0, tiled=True
    )
    flat = blocks.reshape(steps, 2 * piece)
    real_part = jnp.dot(cos_table, flat, precision=lax.Precision.HIGHEST)
    imag_part = -jnp.dot(sin_table, flat, precision=lax.Precision.HIGHEST)
    stacked = jnp.stack([real_part, imag_part], 1).reshape(steps, 2, 2, piece)
    spectrum = lax.all_to_all(stacked, "tm", split_axis=0, concat_axis=3, tiled=True)
    rhat = spectrum[0].reshape(2, 2, rows_dev, cols)
    base = jnp.power(jnp.float32(ALPHA), jnp.float32(1.0) / steps)
    angle = mine * (2.0 * math.pi / steps)
    lam_re = 1.0 - base * jnp.cos(angle)
    lam_im = base * jnp.sin(angle)
    disp_spec = rhat[:, 0]
    right = cmul(disp_spec, lam_re, lam_im) + rhat[:, 1]
    den_re = lam_re * lam_re - lam_im * lam_im + 4.0 * coupling
    den_im = 2.0 * lam_re * lam_im
    magnitude = den_re * den_re + den_im * den_im
    inv_re = den_re / magnitude
    inv_im = -den_im / magnitude
    uhat = cmul(right, inv_re, inv_im)
    for sweep in range(SWEEPS - 1):
        padded = padded_2(uhat, (("rows", 1),), 1)
        uhat = cmul(right + coupling * neighbours(padded), inv_re, inv_im)
    vhat = cmul(uhat, lam_re, lam_im) - disp_spec
    yhat = jnp.stack([uhat, vhat], 1)
    spread = lax.all_to_all(
        yhat.reshape(1, 2, 2, cells), "tm", split_axis=3, concat_axis=0, tiled=True
    )
    real_rows = spread[:, 0].reshape(steps, 2 * piece)
    imag_rows = spread[:, 1].reshape(steps, 2 * piece)
    undo = jnp.power(jnp.float32(ALPHA), -ordinal.astype(jnp.float32) / steps) / steps
    history = jnp.dot(cos_table, real_rows, precision=lax.Precision.HIGHEST) - jnp.dot(
        sin_table, imag_rows, precision=lax.Precision.HIGHEST
    )
    history = (history * undo[:, None]).reshape(steps, 2, piece)
    returned = lax.all_to_all(history, "tm", split_axis=0, concat_axis=2, tiled=True)
    precond = returned[0].reshape(2, rows_dev, cols)
    earlier = shifted(precond, "tm", 1)
    disp_rim = padded_2(precond[0:1], (("rows", 1),), 1)
    laplace = neighbours(disp_rim)[0] - 4.0 * precond[0]
    first = precond[0] - earlier[0] - precond[1]
    second = precond[1] - earlier[1] - coupling * laplace
    image = jnp.stack([first, second])
    inner = jnp.sum(basis[:, :, 0] * image[None], axis=(1, 2, 3))
    count = 2.0 * steps * rows_dev * lax.axis_size("rows") * cols
    squares = jnp.sum(image * image) / count
    local_terms = jnp.concatenate([inner, squares[None]])
    gram = lax.psum(local_terms, ("tm", "rows"))
    return (precond[:, None], image[:, None], gram)


def solution(mesh):
    in_specs = (P(None, "tm", "rows", None), P(None, None, "tm", "rows", None))
    out_specs = (P(None, "tm", "rows", None), P(None, "tm", "rows", None), P())
    return jax.shard_map(
        on_device, mesh=mesh, in_specs=in_specs, out_specs=out_specs, check_vma=False
    )
```

profile of v0, /device:TPU:0, one launch (start us, length us, event | category | flops | bytes accessed | tf_op | source)
XLA Modules:
  0.0 169.4 jit_solution(10434036143663607024)
XLA Ops:
  2.6 19.4 %reduce.4 = f32[4096,2]{1,0:T(8,128)} reduce(f32[4096,1,2]{2,1,0:T(1,128)S(1)} %bitcast.83, f32[]{:T(128)} %broadcast.139), dimensions={1}, to_apply=%bitcast.65.reduce_sub_computation | reduce | bytes 65540
  22.0 3.0 %reshape.138 = f32[16,1,512]{2,1,0:T(1,128)S(1)} reshape(f32[4096,2]{1,0:T(8,128)} %reduce.4) | data formatting | bytes 65536
  25.0 15.5 %all_to_all.63 = f32[16,1,512]{2,1,0:T(1,128)S(1)} all-to-all(f32[16,1,512]{2,1,0:T(1,128)S(1)} %reshape.138), channel_id=1, replica_groups=mesh['tm'=16,'rows'=2] {'tm'}, dimensions={0} | all-to-all | bytes 65536 | tf_op jit(solution)/shard_map/all_to_all | solution.py:61
  41.3 3.4 %reshape.139 = f32[4096,1,2]{2,1,0:T(1,128)S(1)} reshape(f32[16,512]{1,0:T(8,128)S(1)} %reduce.5) | data formatting | bytes 65536
  46.5 3.5 %all-to-all-start.1 = ((f32[16,2,2,256]{3,2,1,0:T(2,128)}), f32[16,2,2,256]{3,2,1,0:T(2,128)S(1)}, u32[]{:S(2)}, u32[]{:S(2)}) async-start(f32[16,2,2,256]{3,2,1,0:T(2,128)} %copy.48), calls=%async_computation.1 | async-start | bytes 131072 | tf_op jit(solution)/shard_map/all_to_all | solution.py:68
  50.2 7.2 %all-to-all-done.1 = f32[16,2,2,256]{3,2,1,0:T(2,128)S(1)} async-done(((f32[16,2,2,256]{3,2,1,0:T(2,128)}), f32[16,2,2,256]{3,2,1,0:T(2,128)S(1)}, u32[]{:S(2)}, u32[]{:S(2)}) %all-to-all-start.1) | async-done | bytes 65568 | tf_op jit(solution)/shard_map/all_to_all | solution.py:68
  57.6 1.3 collective-permute-start
  58.9 3.0 %collective-permute-start.1 = (f32[2,1,512]{2,1,0:T(1,128)S(1)}, f32[2,1,512]{2,1,0:T(1,128)S(1)}, u32[]{:S(2)}, u32[]{:S(2)}) collective-permute-start(f32[2,1,512]{2,1,0:T(1,128)S(1)} %get-tuple-element.26), channel_id=1, source_target_pairs={{0,1},{2,3},{4,5},{6,7},{8,9},{10,11},{12,13},{14,15},{16,17},{18,... | collective-permute-start | bytes 12296 | tf_op jit(solution)/shard_map/ppermute | solution.py:18
  62.9 1.3 collective-permute-start.2
  64.2 3.0 %collective-permute-start.3 = (f32[2,1,512]{2,1,0:T(1,128)S(1)}, f32[2,1,512]{2,1,0:T(1,128)S(1)}, u32[]{:S(2)}, u32[]{:S(2)}) collective-permute-start(f32[2,1,512]{2,1,0:T(1,128)S(1)} %get-tuple-element.22), channel_id=1, source_target_pairs={{0,1},{2,3},{4,5},{6,7},{8,9},{10,11},{12,13},{14,15},{16,17},{18,... | collective-permute-start | bytes 12296 | tf_op jit(solution)/shard_map/ppermute | solution.py:18
  68.1 1.3 collective-permute-start.4
  69.4 3.2 %collective-permute-start.5 = (f32[2,1,512]{2,1,0:T(1,128)S(1)}, f32[2,1,512]{2,1,0:T(1,128)S(1)}, u32[]{:S(2)}, u32[]{:S(2)}) collective-permute-start(f32[2,1,512]{2,1,0:T(1,128)S(1)} %get-tuple-element.18), channel_id=1, source_target_pairs={{0,1},{2,3},{4,5},{6,7},{8,9},{10,11},{12,13},{14,15},{16,17},{18,... | collective-permute-start | bytes 12296 | tf_op jit(solution)/shard_map/ppermute | solution.py:18
  73.5 4.4 %copy.51 = f32[1,2,2,4096]{2,1,0,3:T(2,128)} copy(f32[1,2,2,4096]{3,1,2,0:T(2,128)S(1)} %pad_maximum_fusion.1) | data formatting | bytes 131072 | tf_op jit(solution)/shard_map/stack | solution.py:86
  77.9 8.1 %reshape.140 = f32[16,1,1024]{2,1,0:T(1,128)} reshape(f32[4096,1,2,2]{3,2,1,0:T(2,128)} %bitcast.81) | data formatting | bytes 131072
  86.0 3.5 %all-to-all-start.2 = ((f32[16,1,1024]{2,1,0:T(1,128)}), f32[16,1,1024]{2,1,0:T(1,128)S(1)}, u32[]{:S(2)}, u32[]{:S(2)}) async-start(f32[16,1,1024]{2,1,0:T(1,128)} %reshape.140), calls=%async_computation.2 | async-start | bytes 131072 | tf_op jit(solution)/shard_map/all_to_all | solution.py:87
  89.5 7.5 %all-to-all-done.2 = f32[16,1,1024]{2,1,0:T(1,128)S(1)} async-done(((f32[16,1,1024]{2,1,0:T(1,128)}), f32[16,1,1024]{2,1,0:T(1,128)S(1)}, u32[]{:S(2)}, u32[]{:S(2)}) %all-to-all-start.2) | async-done | bytes 65568 | tf_op jit(solution)/shard_map/all_to_all | solution.py:87
  97.8 7.7 %reshape.141 = f32[4096,1,2,2]{3,2,1,0:T(2,128)} reshape(f32[16,1024]{1,0:T(8,128)S(1)} %reduce.6) | data formatting | bytes 131072
  105.6 3.6 %copy.57 = f32[1,2,2,16,256]{4,3,2,1,0:T(8,128)S(1)} copy(f32[1,2,2,16,256]{2,1,4,3,0:T(2,128)} %bitcast.82) | data formatting | bytes 131072 | tf_op jit(solution)/shard_map/all_to_all | solution.py:87
  109.7 10.0 %all_to_all.64 = f32[16,2,256]{2,1,0:T(2,128)S(1)} all-to-all(f32[16,2,256]{2,1,0:T(2,128)S(1)} %reshape.134), channel_id=1, replica_groups=mesh['tm'=16,'rows'=2] {'tm'}, dimensions={0} | all-to-all | bytes 65536 | tf_op jit(solution)/shard_map/all_to_all | solution.py:97
  119.8 2.6 %collective-permute-start.6 = (f32[2,8,512]{2,1,0:T(8,128)S(1)}, f32[2,8,512]{2,1,0:T(8,128)S(1)}, u32[]{:S(2)}, u32[]{:S(2)}) collective-permute-start(f32[2,8,512]{2,1,0:T(8,128)S(1)} %reshape_squeeze.15), channel_id=1, source_target_pairs={{0,2},{2,4},{4,6},{6,8},{8,10},{10,12},{12,14},{14,16},{16,18},{18... | collective-permute-start | bytes 98312 | tf_op jit(solution)/shard_map/ppermute | solution.py:27
  122.4 1.3 collective-permute-start.7
  123.7 3.0 %collective-permute-start.8 = (f32[1,1,512]{2,1,0:T(1,128)S(1)}, f32[1,1,512]{2,1,0:T(1,128)S(1)}, u32[]{:S(2)}, u32[]{:S(2)}) collective-permute-start(f32[1,1,512]{2,1,0:T(1,128)S(1)} %get-tuple-element.30), channel_id=1, source_target_pairs={{0,1},{2,3},{4,5},{6,7},{8,9},{10,11},{12,13},{14,15},{16,17},{18,... | collective-permute-start | bytes 6152 | tf_op jit(solution)/shard_map/ppermute | solution.py:18
  127.7 1.2 pad_maximum_fusion.18
  130.4 39.0 %psum.7 = f32[5]{0:T(128)} all-reduce(f32[5]{0:T(128)S(1)} %pad_maximum_fusion.21), channel_id=1, replica_groups=mesh['tm'=16,'rows'=2] {'tm','rows'}, use_global_device_ids=true, to_apply=%region_2.3 | all-reduce | flops 5 | bytes 40 | tf_op jit(solution)/shard_map/psum | solution.py:109
  (66 shorter events, 10.2 us)
Async XLA Ops:
  46.5 11.0 %all-to-all-start.1 = ((f32[16,2,2,256]{3,2,1,0:T(2,128)}), f32[16,2,2,256]{3,2,1,0:T(2,128)S(1)}, u32[]{:S(2)}, u32[]{:S(2)}) async-start(f32[16,2,2,256]{3,2,1,0:T(2,128)} %copy.48), calls=%async_computation.1 | async-start | bytes 131072 | tf_op jit(solution)/shard_map/all_to_all | solution.py:68
  57.6 4.3 %collective-permute-start = (f32[2,1,512]{2,1,0:T(1,128)S(1)}, f32[2,1,512]{2,1,0:T(1,128)S(1)}, u32[]{:S(2)}, u32[]{:S(2)}) collective-permute-start(f32[2,1,512]{2,1,0:T(1,128)S(1)} %get-tuple-element.25), channel_id=1, source_target_pairs={{1,0},{3,2},{5,4},{7,6},{9,8},{11,10},{13,12},{15,14},{17,16},{19,... | collective-permute-start | bytes 12296 | tf_op jit(solution)/shard_map/ppermute | solution.py:19
  58.9 3.8 %collective-permute-start.1 = (f32[2,1,512]{2,1,0:T(1,128)S(1)}, f32[2,1,512]{2,1,0:T(1,128)S(1)}, u32[]{:S(2)}, u32[]{:S(2)}) collective-permute-start(f32[2,1,512]{2,1,0:T(1,128)S(1)} %get-tuple-element.26), channel_id=1, source_target_pairs={{0,1},{2,3},{4,5},{6,7},{8,9},{10,11},{12,13},{14,15},{16,17},{18,... | collective-permute-start | bytes 12296 | tf_op jit(solution)/shard_map/ppermute | solution.py:18
  62.9 4.3 %collective-permute-start.2 = (f32[2,1,512]{2,1,0:T(1,128)S(1)}, f32[2,1,512]{2,1,0:T(1,128)S(1)}, u32[]{:S(2)}, u32[]{:S(2)}) collective-permute-start(f32[2,1,512]{2,1,0:T(1,128)S(1)} %get-tuple-element.21), channel_id=1, source_target_pairs={{1,0},{3,2},{5,4},{7,6},{9,8},{11,10},{13,12},{15,14},{17,16},{19,... | collective-permute-start | bytes 12296 | tf_op jit(solution)/shard_map/ppermute | solution.py:19
  64.2 3.8 %collective-permute-start.3 = (f32[2,1,512]{2,1,0:T(1,128)S(1)}, f32[2,1,512]{2,1,0:T(1,128)S(1)}, u32[]{:S(2)}, u32[]{:S(2)}) collective-permute-start(f32[2,1,512]{2,1,0:T(1,128)S(1)} %get-tuple-element.22), channel_id=1, source_target_pairs={{0,1},{2,3},{4,5},{6,7},{8,9},{10,11},{12,13},{14,15},{16,17},{18,... | collective-permute-start | bytes 12296 | tf_op jit(solution)/shard_map/ppermute | solution.py:18
  68.1 4.5 %collective-permute-start.4 = (f32[2,1,512]{2,1,0:T(1,128)S(1)}, f32[2,1,512]{2,1,0:T(1,128)S(1)}, u32[]{:S(2)}, u32[]{:S(2)}) collective-permute-start(f32[2,1,512]{2,1,0:T(1,128)S(1)} %get-tuple-element.17), channel_id=1, source_target_pairs={{1,0},{3,2},{5,4},{7,6},{9,8},{11,10},{13,12},{15,14},{17,16},{19,... | collective-permute-start | bytes 12296 | tf_op jit(solution)/shard_map/ppermute | solution.py:19
  69.4 3.8 %collective-permute-start.5 = (f32[2,1,512]{2,1,0:T(1,128)S(1)}, f32[2,1,512]{2,1,0:T(1,128)S(1)}, u32[]{:S(2)}, u32[]{:S(2)}) collective-permute-start(f32[2,1,512]{2,1,0:T(1,128)S(1)} %get-tuple-element.18), channel_id=1, source_target_pairs={{0,1},{2,3},{4,5},{6,7},{8,9},{10,11},{12,13},{14,15},{16,17},{18,... | collective-permute-start | bytes 12296 | tf_op jit(solution)/shard_map/ppermute | solution.py:18
  86.0 11.0 %all-to-all-start.2 = ((f32[16,1,1024]{2,1,0:T(1,128)}), f32[16,1,1024]{2,1,0:T(1,128)S(1)}, u32[]{:S(2)}, u32[]{:S(2)}) async-start(f32[16,1,1024]{2,1,0:T(1,128)} %reshape.140), calls=%async_computation.2 | async-start | bytes 131072 | tf_op jit(solution)/shard_map/all_to_all | solution.py:87
  105.6 24.0 %copy-start = (f32[4,2,1,8,512]{4,3,2,1,0:T(8,128)S(1)}, f32[4,2,1,8,512]{4,3,2,1,0:T(8,128)}, u32[]{:S(2)}) copy-start(f32[4,2,1,8,512]{4,3,2,1,0:T(8,128)} %param.3) | copy-start | bytes 393220
  119.8 7.8 %collective-permute-start.6 = (f32[2,8,512]{2,1,0:T(8,128)S(1)}, f32[2,8,512]{2,1,0:T(8,128)S(1)}, u32[]{:S(2)}, u32[]{:S(2)}) collective-permute-start(f32[2,8,512]{2,1,0:T(8,128)S(1)} %reshape_squeeze.15), channel_id=1, source_target_pairs={{0,2},{2,4},{4,6},{6,8},{8,10},{10,12},{12,14},{14,16},{16,18},{18... | collective-permute-start | bytes 98312 | tf_op jit(solution)/shard_map/ppermute | solution.py:27
  122.4 4.4 %collective-permute-start.7 = (f32[1,1,512]{2,1,0:T(1,128)S(1)}, f32[1,1,512]{2,1,0:T(1,128)S(1)}, u32[]{:S(2)}, u32[]{:S(2)}) collective-permute-start(f32[1,1,512]{2,1,0:T(1,128)S(1)} %get-tuple-element.29), channel_id=1, source_target_pairs={{1,0},{3,2},{5,4},{7,6},{9,8},{11,10},{13,12},{15,14},{17,16},{19,... | collective-permute-start | bytes 6152 | tf_op jit(solution)/shard_map/ppermute | solution.py:19
  123.7 3.8 %collective-permute-start.8 = (f32[1,1,512]{2,1,0:T(1,128)S(1)}, f32[1,1,512]{2,1,0:T(1,128)S(1)}, u32[]{:S(2)}, u32[]{:S(2)}) collective-permute-start(f32[1,1,512]{2,1,0:T(1,128)S(1)} %get-tuple-element.30), channel_id=1, source_target_pairs={{0,1},{2,3},{4,5},{6,7},{8,9},{10,11},{12,13},{14,15},{16,17},{18,... | collective-permute-start | bytes 6152 | tf_op jit(solution)/shard_map/ppermute | solution.py:18
where the time goes:
time: 170 us; the launch traced here: 169 us
  blocking collectives  64.5 us (38%)
  local copies, waits for them, and re-layouts  33.7 us (20%)
  starting transfers between devices  27 us (16%)
  other arithmetic  23.6 us (14%)
  waiting for transfers between devices  17.7 us (10%)
  between operations  2.06 us (1%)
    psum x1, blocking collectives, on_device(): gram = lax.psum(local_terms, ('tm', 'rows'))  39 us
    unnamed x10, local copies, waits for them, and re-layouts  22.8 us
    unnamed x1, other arithmetic  19.4 us
    all_to_all x1, blocking collectives, on_device(): lax.all_to_all(scaled.reshape(1, 2, cells), 'tm', split_axis=2, concat_ax...  15.5 us
    ppermute x4, starting transfers between devices, padded_2(): before = lax.ppermute(last, axis, up)  12.3 us
    all_to_all x1, blocking collectives, on_device(): lax.all_to_all(history, 'tm', split_axis=0, concat_axis=2, tiled=True)  9.98 us
    all_to_all x1, waiting for transfers between devices, on_device(): lax.all_to_all(yhat.reshape(1, 2, 2, cells), 'tm', split_axis=3, concat_a...  7.49 us
    all_to_all x1, waiting for transfers between devices, on_device(): lax.all_to_all(stacked, 'tm', split_axis=0, concat_axis=3, tiled=True)  7.25 us
  transfers between devices with their start and end apart: 11, of which 6 were waited for; matrix products, arithmetic and copies ran while one was open for 0% of the time, Pallas kernels for 0%

commit v1 on v0

--- a/solution.py
+++ b/solution.py
@@ -84,9 +84,11 @@
         uhat = cmul(right + coupling * neighbours(padded), inv_re, inv_im)
     vhat = cmul(uhat, lam_re, lam_im) - disp_spec
     yhat = jnp.stack([uhat, vhat], 1)
-    spread = lax.all_to_all(
-        yhat.reshape(1, 2, 2, cells), "tm", split_axis=3, concat_axis=0, tiled=True
-    )
+    part = yhat.reshape(1, 2, 2, cells)
+    devices = lax.axis_size("tm")
+    pieces = jnp.stack(jnp.split(part, devices, axis=3), axis=0)
+    pieces = lax.all_to_all(pieces, "tm", split_axis=0, concat_axis=0)
+    spread = jnp.concatenate(pieces, axis=0)
     real_rows = spread[:, 0].reshape(steps, 2 * piece)
     imag_rows = spread[:, 1].reshape(steps, 2 * piece)
     undo = jnp.power(jnp.float32(ALPHA), -ordinal.astype(jnp.float32) / steps) / steps

time: 170 us -> 155 us (0.912)
  local copies, waits for them, and re-layouts: 33.7 us -> 19.5 us
    unnamed x10 -> x24, local copies, waits for them, and re-layouts: 22.8 us -> 15.9 us
    another operation x3, local copies, waits for them, and re-layouts: 4.46 us -> 0.07 us  [on_device(): yhat = jnp.stack([uhat, vhat], 1)]
    all_to_all x1 -> x0, local copies, waits for them, and re-layouts: 3.58 us -> none  [on_device(): lax.all_to_all(yhat.reshape(1, 2, 2, cells), 'tm', split_axis=3, concat_a...]
where the time goes in v1:
time: 155 us; the launch traced here: 154 us
  blocking collectives  64.6 us (42%)
  starting transfers between devices  26.8 us (17%)
  other arithmetic  22.8 us (15%)
  local copies, waits for them, and re-layouts  19.5 us (13%)
  waiting for transfers between devices  17.9 us (12%)
  between operations  2 us (1%)
    psum x1, blocking collectives, on_device(): gram = lax.psum(local_terms, ('tm', 'rows'))  39 us
    unnamed x1, other arithmetic  19.4 us
    unnamed x24, local copies, waits for them, and re-layouts  15.9 us
    all_to_all x1, blocking collectives, on_device(): lax.all_to_all(scaled.reshape(1, 2, cells), 'tm', split_axis=2, concat_ax...  15.5 us
    ppermute x4, starting transfers between devices, padded_2(): before = lax.ppermute(last, axis, up)  12.1 us
    all_to_all x1, blocking collectives, on_device(): lax.all_to_all(history, 'tm', split_axis=0, concat_axis=2, tiled=True)  9.98 us
    all_to_all x1, waiting for transfers between devices, on_device(): pieces = lax.all_to_all(pieces, 'tm', split_axis=0, concat_axis=0)  7.49 us
    all_to_all x1, waiting for transfers between devices, on_device(): lax.all_to_all(stacked, 'tm', split_axis=0, concat_axis=3, tiled=True)  7.25 us
  transfers between devices with their start and end apart: 11, of which 6 were waited for; matrix products, arithmetic and copies ran while one was open for 0% of the time, Pallas kernels for 0%

profile of v1, /device:TPU:0, one launch (start us, length us, event | category | flops | bytes accessed | tf_op | source)
XLA Modules:
  0.0 154.4 jit_solution(12353905935334969767)
XLA Ops:
  2.6 19.4 %reduce.8 = f32[4096,2]{1,0:T(8,128)} reduce(f32[4096,1,2]{2,1,0:T(1,128)S(1)} %bitcast.136, f32[]{:T(128)} %broadcast.141), dimensions={1}, to_apply=%bitcast.122.reduce_sub_computation | reduce | bytes 65540
  22.0 3.0 %reshape.144 = f32[16,1,512]{2,1,0:T(1,128)S(1)} reshape(f32[4096,2]{1,0:T(8,128)} %reduce.8) | data formatting | bytes 65536
  25.0 15.5 %all_to_all.50 = f32[16,1,512]{2,1,0:T(1,128)S(1)} all-to-all(f32[16,1,512]{2,1,0:T(1,128)S(1)} %reshape.144), channel_id=1, replica_groups=mesh['tm'=16,'rows'=2] {'tm'}, dimensions={0} | all-to-all | bytes 65536 | tf_op jit(solution)/shard_map/all_to_all | solution.py:61
  41.3 3.4 %reshape.145 = f32[4096,1,2]{2,1,0:T(1,128)S(1)} reshape(f32[16,512]{1,0:T(8,128)S(1)} %reduce.9) | data formatting | bytes 65536
  46.5 3.5 %all-to-all-start.1 = ((f32[16,2,2,256]{3,2,1,0:T(2,128)}), f32[16,2,2,256]{3,2,1,0:T(2,128)S(1)}, u32[]{:S(2)}, u32[]{:S(2)}) async-start(f32[16,2,2,256]{3,2,1,0:T(2,128)} %copy.25), calls=%async_computation.1 | async-start | bytes 131072 | tf_op jit(solution)/shard_map/all_to_all | solution.py:68
  50.2 7.2 %all-to-all-done.1 = f32[16,2,2,256]{3,2,1,0:T(2,128)S(1)} async-done(((f32[16,2,2,256]{3,2,1,0:T(2,128)}), f32[16,2,2,256]{3,2,1,0:T(2,128)S(1)}, u32[]{:S(2)}, u32[]{:S(2)}) %all-to-all-start.1) | async-done | bytes 65568 | tf_op jit(solution)/shard_map/all_to_all | solution.py:68
  57.6 1.3 collective-permute-start
  58.9 3.0 %collective-permute-start.1 = (f32[2,1,512]{2,1,0:T(1,128)S(1)}, f32[2,1,512]{2,1,0:T(1,128)S(1)}, u32[]{:S(2)}, u32[]{:S(2)}) collective-permute-start(f32[2,1,512]{2,1,0:T(1,128)S(1)} %get-tuple-element.26), channel_id=1, source_target_pairs={{0,1},{2,3},{4,5},{6,7},{8,9},{10,11},{12,13},{14,15},{16,17},{18,... | collective-permute-start | bytes 12296 | tf_op jit(solution)/shard_map/ppermute | solution.py:18
  62.0 0.8 collective-permute-done.1
  62.9 1.3 collective-permute-start.2
  64.2 3.0 %collective-permute-start.3 = (f32[2,1,512]{2,1,0:T(1,128)S(1)}, f32[2,1,512]{2,1,0:T(1,128)S(1)}, u32[]{:S(2)}, u32[]{:S(2)}) collective-permute-start(f32[2,1,512]{2,1,0:T(1,128)S(1)} %get-tuple-element.22), channel_id=1, source_target_pairs={{0,1},{2,3},{4,5},{6,7},{8,9},{10,11},{12,13},{14,15},{16,17},{18,... | collective-permute-start | bytes 12296 | tf_op jit(solution)/shard_map/ppermute | solution.py:18
  67.2 0.8 collective-permute-done.3
  68.1 1.3 collective-permute-start.4
  69.4 3.0 %collective-permute-start.5 = (f32[2,1,512]{2,1,0:T(1,128)S(1)}, f32[2,1,512]{2,1,0:T(1,128)S(1)}, u32[]{:S(2)}, u32[]{:S(2)}) collective-permute-start(f32[2,1,512]{2,1,0:T(1,128)S(1)} %get-tuple-element.18), channel_id=1, source_target_pairs={{0,1},{2,3},{4,5},{6,7},{8,9},{10,11},{12,13},{14,15},{16,17},{18,... | collective-permute-start | bytes 12296 | tf_op jit(solution)/shard_map/ppermute | solution.py:18
  72.5 0.8 collective-permute-done.5
  83.0 3.5 %all-to-all-start.2 = ((f32[16,1,2,2,256]{4,2,3,1,0:T(2,128)}), f32[16,1,2,2,256]{4,2,3,1,0:T(2,128)S(1)}, u32[]{:S(2)}, u32[]{:S(2)}) async-start(f32[16,1,2,2,256]{4,2,3,1,0:T(2,128)} %constant_dynamic-update-slice_fusion.2), calls=%async_computation.2 | async-start | bytes 131072 | tf_op jit(solution)/shard_map/all_to_all | solution.py:90
  86.5 7.5 %all-to-all-done.2 = f32[16,1,2,2,256]{4,2,3,1,0:T(2,128)S(1)} async-done(((f32[16,1,2,2,256]{4,2,3,1,0:T(2,128)}), f32[16,1,2,2,256]{4,2,3,1,0:T(2,128)S(1)}, u32[]{:S(2)}, u32[]{:S(2)}) %all-to-all-start.2) | async-done | bytes 65568 | tf_op jit(solution)/shard_map/all_to_all | solution.py:90
  94.7 10.0 %all_to_all.51 = f32[16,2,256]{2,1,0:T(2,128)S(1)} all-to-all(f32[16,2,256]{2,1,0:T(2,128)S(1)} %reshape.138), channel_id=1, replica_groups=mesh['tm'=16,'rows'=2] {'tm'}, dimensions={0} | all-to-all | bytes 65536 | tf_op jit(solution)/shard_map/all_to_all | solution.py:99
  104.8 2.6 %collective-permute-start.6 = (f32[2,8,512]{2,1,0:T(8,128)S(1)}, f32[2,8,512]{2,1,0:T(8,128)S(1)}, u32[]{:S(2)}, u32[]{:S(2)}) collective-permute-start(f32[2,8,512]{2,1,0:T(8,128)S(1)} %reshape_squeeze.15), channel_id=1, source_target_pairs={{0,2},{2,4},{4,6},{6,8},{8,10},{10,12},{12,14},{14,16},{16,18},{18... | collective-permute-start | bytes 98312 | tf_op jit(solution)/shard_map/ppermute | solution.py:27
  107.4 1.3 collective-permute-start.7
  108.7 3.0 %collective-permute-start.8 = (f32[1,1,512]{2,1,0:T(1,128)S(1)}, f32[1,1,512]{2,1,0:T(1,128)S(1)}, u32[]{:S(2)}, u32[]{:S(2)}) collective-permute-start(f32[1,1,512]{2,1,0:T(1,128)S(1)} %get-tuple-element.30), channel_id=1, source_target_pairs={{0,1},{2,3},{4,5},{6,7},{8,9},{10,11},{12,13},{14,15},{16,17},{18,... | collective-permute-start | bytes 6152 | tf_op jit(solution)/shard_map/ppermute | solution.py:18
  111.7 0.8 collective-permute-done.8
  112.6 1.2 pad_maximum_fusion.17
  115.3 39.0 %psum.7 = f32[5]{0:T(128)} all-reduce(f32[5]{0:T(128)S(1)} %pad_maximum_fusion.20), channel_id=1, replica_groups=mesh['tm'=16,'rows'=2] {'tm','rows'}, use_global_device_ids=true, to_apply=%region_2.3 | all-reduce | flops 5 | bytes 40 | tf_op jit(solution)/shard_map/psum | solution.py:111
  (76 shorter events, 16.1 us)
Async XLA Ops:
  45.3 69.2 %copy-start = (f32[4,2,1,8,512]{4,3,2,1,0:T(8,128)S(1)}, f32[4,2,1,8,512]{4,3,2,1,0:T(8,128)}, u32[]{:S(2)}) copy-start(f32[4,2,1,8,512]{4,3,2,1,0:T(8,128)} %param.3) | copy-start | bytes 393220
  46.5 11.0 %all-to-all-start.1 = ((f32[16,2,2,256]{3,2,1,0:T(2,128)}), f32[16,2,2,256]{3,2,1,0:T(2,128)S(1)}, u32[]{:S(2)}, u32[]{:S(2)}) async-start(f32[16,2,2,256]{3,2,1,0:T(2,128)} %copy.25), calls=%async_computation.1 | async-start | bytes 131072 | tf_op jit(solution)/shard_map/all_to_all | solution.py:68
  57.6 4.3 %collective-permute-start = (f32[2,1,512]{2,1,0:T(1,128)S(1)}, f32[2,1,512]{2,1,0:T(1,128)S(1)}, u32[]{:S(2)}, u32[]{:S(2)}) collective-permute-start(f32[2,1,512]{2,1,0:T(1,128)S(1)} %get-tuple-element.25), channel_id=1, source_target_pairs={{1,0},{3,2},{5,4},{7,6},{9,8},{11,10},{13,12},{15,14},{17,16},{19,... | collective-permute-start | bytes 12296 | tf_op jit(solution)/shard_map/ppermute | solution.py:19
  58.9 3.8 %collective-permute-start.1 = (f32[2,1,512]{2,1,0:T(1,128)S(1)}, f32[2,1,512]{2,1,0:T(1,128)S(1)}, u32[]{:S(2)}, u32[]{:S(2)}) collective-permute-start(f32[2,1,512]{2,1,0:T(1,128)S(1)} %get-tuple-element.26), channel_id=1, source_target_pairs={{0,1},{2,3},{4,5},{6,7},{8,9},{10,11},{12,13},{14,15},{16,17},{18,... | collective-permute-start | bytes 12296 | tf_op jit(solution)/shard_map/ppermute | solution.py:18
  62.9 4.3 %collective-permute-start.2 = (f32[2,1,512]{2,1,0:T(1,128)S(1)}, f32[2,1,512]{2,1,0:T(1,128)S(1)}, u32[]{:S(2)}, u32[]{:S(2)}) collective-permute-start(f32[2,1,512]{2,1,0:T(1,128)S(1)} %get-tuple-element.21), channel_id=1, source_target_pairs={{1,0},{3,2},{5,4},{7,6},{9,8},{11,10},{13,12},{15,14},{17,16},{19,... | collective-permute-start | bytes 12296 | tf_op jit(solution)/shard_map/ppermute | solution.py:19
  64.2 3.8 %collective-permute-start.3 = (f32[2,1,512]{2,1,0:T(1,128)S(1)}, f32[2,1,512]{2,1,0:T(1,128)S(1)}, u32[]{:S(2)}, u32[]{:S(2)}) collective-permute-start(f32[2,1,512]{2,1,0:T(1,128)S(1)} %get-tuple-element.22), channel_id=1, source_target_pairs={{0,1},{2,3},{4,5},{6,7},{8,9},{10,11},{12,13},{14,15},{16,17},{18,... | collective-permute-start | bytes 12296 | tf_op jit(solution)/shard_map/ppermute | solution.py:18
  68.1 4.3 %collective-permute-start.4 = (f32[2,1,512]{2,1,0:T(1,128)S(1)}, f32[2,1,512]{2,1,0:T(1,128)S(1)}, u32[]{:S(2)}, u32[]{:S(2)}) collective-permute-start(f32[2,1,512]{2,1,0:T(1,128)S(1)} %get-tuple-element.17), channel_id=1, source_target_pairs={{1,0},{3,2},{5,4},{7,6},{9,8},{11,10},{13,12},{15,14},{17,16},{19,... | collective-permute-start | bytes 12296 | tf_op jit(solution)/shard_map/ppermute | solution.py:19
  69.4 3.8 %collective-permute-start.5 = (f32[2,1,512]{2,1,0:T(1,128)S(1)}, f32[2,1,512]{2,1,0:T(1,128)S(1)}, u32[]{:S(2)}, u32[]{:S(2)}) collective-permute-start(f32[2,1,512]{2,1,0:T(1,128)S(1)} %get-tuple-element.18), channel_id=1, source_target_pairs={{0,1},{2,3},{4,5},{6,7},{8,9},{10,11},{12,13},{14,15},{16,17},{18,... | collective-permute-start | bytes 12296 | tf_op jit(solution)/shard_map/ppermute | solution.py:18
  83.0 11.0 %all-to-all-start.2 = ((f32[16,1,2,2,256]{4,2,3,1,0:T(2,128)}), f32[16,1,2,2,256]{4,2,3,1,0:T(2,128)S(1)}, u32[]{:S(2)}, u32[]{:S(2)}) async-start(f32[16,1,2,2,256]{4,2,3,1,0:T(2,128)} %constant_dynamic-update-slice_fusion.2), calls=%async_computation.2 | async-start | bytes 131072 | tf_op jit(solution)/shard_map/all_to_all | solution.py:90
  104.8 7.8 %collective-permute-start.6 = (f32[2,8,512]{2,1,0:T(8,128)S(1)}, f32[2,8,512]{2,1,0:T(8,128)S(1)}, u32[]{:S(2)}, u32[]{:S(2)}) collective-permute-start(f32[2,8,512]{2,1,0:T(8,128)S(1)} %reshape_squeeze.15), channel_id=1, source_target_pairs={{0,2},{2,4},{4,6},{6,8},{8,10},{10,12},{12,14},{14,16},{16,18},{18... | collective-permute-start | bytes 98312 | tf_op jit(solution)/shard_map/ppermute | solution.py:27
  107.4 4.4 %collective-permute-start.7 = (f32[1,1,512]{2,1,0:T(1,128)S(1)}, f32[1,1,512]{2,1,0:T(1,128)S(1)}, u32[]{:S(2)}, u32[]{:S(2)}) collective-permute-start(f32[1,1,512]{2,1,0:T(1,128)S(1)} %get-tuple-element.29), channel_id=1, source_target_pairs={{1,0},{3,2},{5,4},{7,6},{9,8},{11,10},{13,12},{15,14},{17,16},{19,... | collective-permute-start | bytes 6152 | tf_op jit(solution)/shard_map/ppermute | solution.py:19
  108.7 3.8 %collective-permute-start.8 = (f32[1,1,512]{2,1,0:T(1,128)S(1)}, f32[1,1,512]{2,1,0:T(1,128)S(1)}, u32[]{:S(2)}, u32[]{:S(2)}) collective-permute-start(f32[1,1,512]{2,1,0:T(1,128)S(1)} %get-tuple-element.30), channel_id=1, source_target_pairs={{0,1},{2,3},{4,5},{6,7},{8,9},{10,11},{12,13},{14,15},{16,17},{18,... | collective-permute-start | bytes 6152 | tf_op jit(solution)/shard_map/ppermute | solution.py:18
